TPU v7x, 32 devices: a whole 2x2x4 slice. The times are simulated.
32 devices in a mesh: rep: 8 (over y, x, core), grp: 4 (over z).
Axes of the slice: x: 2, y: 2, z: 4, core: 2. Of those that a mesh axis runs over, the one named last changes fastest.
Arguments:
- tokens: bfloat16 [8, 1024, 512], P('rep', 'grp'), may hold values from -6 to 6
- segments: int32 [8, 1024], P('rep', 'grp'), may hold values from 0 to 1024, as said below
- positions: int32 [8, 1024], P('rep', 'grp'), may hold values from 0 to 1023, as said below
- norm1_gain: bfloat16 [512], P('grp'), may hold values from 0.5 to 1.5
- w_query: bfloat16 [512, 512], P('grp'), may hold values from -0.25 to 0.25
- w_key: bfloat16 [512, 512], P('grp'), may hold values from -0.25 to 0.25
- w_value: bfloat16 [512, 512], P('grp'), may hold values from -0.25 to 0.25
- w_out: bfloat16 [512, 512], P('grp'), may hold values from -1 to 1
- norm2_gain: bfloat16 [512], P('grp'), may hold values from 0.5 to 1.5
- w_gate: bfloat16 [512, 1376], P('grp'), may hold values from -0.25 to 0.25
- w_up: bfloat16 [512, 1376], P('grp'), may hold values from -0.25 to 0.25
- w_down: bfloat16 [1376, 512], P('grp'), may hold values from -0.15625 to 0.15625
- cotangent: bfloat16 [8, 1024, 512], P('rep', 'grp'), may hold values from -6 to 6
Outputs:
- output: bfloat16 [8, 1024, 512], P('rep', 'grp')
- input_grad: float32 [8, 1024, 512], P('rep', 'grp')
- grad_norm1: float32 [512], P('grp')
- grad_query: float32 [512, 512], P('grp')
- grad_key: float32 [512, 512], P('grp')
- grad_value: float32 [512, 512], P('grp')
- grad_out: float32 [512, 512], P('grp')
- grad_norm2: float32 [512], P('grp')
- grad_gate: float32 [512, 1376], P('grp')
- grad_up: float32 [512, 1376], P('grp')
- grad_down: float32 [1376, 512], P('grp')
Inputs may be any that keep to these rules, and one draw needn't show every extreme that they name: `segments`: in each sequence the documents are runs of consecutive tokens numbered 1, 2, 3 in order; tokens after the last document, if any, are padding numbered 0. `positions`: A token's index in its sequence minus the index of the first token of its run (its document, or the padding).
All inputs are finite; a program needn't handle non-finite values.
Results may differ from a plain program's by a relative error of at most 0.019.
Values may be sent and summed in bfloat16 or wider, within the bound.
No kernel may reach another device: no remote copies, remote signals or barrier semaphores. Data moves between devices by JAX's collectives and lax.ppermute only.
A program may use at most 64 MiB of HBM per device.

v0:
```python
import jax
import jax.numpy as jnp
from jax import lax
from jax.sharding import PartitionSpec as P

D = 512
H = 8
KV = 8
HD = 64
EPSILON = 1e-05
NEGATIVE = -1e30


def norm_scale(values):
    return lax.rsqrt(jnp.mean(values * values, axis=-1, keepdims=True) + EPSILON)


def rotation_tables(positions, width):
    halves = width // 2
    frequency = 10000.0 ** (-2.0 * jnp.arange(halves, dtype=jnp.float32) / width)
    angles = positions.astype(jnp.float32)[..., None, None] * frequency
    return (jnp.cos(angles), jnp.sin(angles))


def rotate(values, cosine, sines):
    halves = values.shape[-1] // 2
    first_half = values[..., :halves]
    second_half = values[..., halves:]
    return jnp.concatenate(
        [first_half * cosine - second_half * sines, second_half * cosine + first_half * sines],
        axis=-1,
    )


def rotate_back(gradient, cosine, sines):
    halves = gradient.shape[-1] // 2
    first_half = gradient[..., :halves]
    second_half = gradient[..., halves:]
    return jnp.concatenate(
        [first_half * cosine + second_half * sines, second_half * cosine - first_half * sines],
        axis=-1,
    )


def contract_rows(left, right):
    return lax.dot_general(
        left, right, (((0,), (0,)), ((), ())), preferred_element_type=jnp.float32
    )


def against(left, right):
    return lax.dot_general(
        left, right, (((1,), (1,)), ((), ())), preferred_element_type=jnp.float32
    )


def fetch_attention(norm1_gain, w_query, w_key, w_value, w_out):
    return (
        lax.all_gather(norm1_gain, "grp", axis=0, tiled=True),
        lax.all_gather(w_query, "grp", axis=0, tiled=True),
        lax.all_gather(w_key, "grp", axis=0, tiled=True),
        lax.all_gather(w_value, "grp", axis=0, tiled=True),
        lax.all_gather(w_out, "grp", axis=0, tiled=True),
    )


def fetch_mlp(norm2_gain, w_gate, w_up, w_down):
    return (
        lax.all_gather(norm2_gain, "grp", axis=0, tiled=True),
        lax.all_gather(w_gate, "grp", axis=0, tiled=True),
        lax.all_gather(w_up, "grp", axis=0, tiled=True),
        lax.all_gather(w_down, "grp", axis=0, tiled=True),
    )


def replica_all(parts):
    return (
        lax.psum(parts[0].astype(jnp.bfloat16), "rep").astype(jnp.float32),
        lax.psum(parts[1].astype(jnp.bfloat16), "rep").astype(jnp.float32),
        lax.psum(parts[2].astype(jnp.bfloat16), "rep").astype(jnp.float32),
        lax.psum(parts[3].astype(jnp.bfloat16), "rep").astype(jnp.float32),
        lax.psum(parts[4].astype(jnp.bfloat16), "rep").astype(jnp.float32),
        lax.psum(parts[5].astype(jnp.bfloat16), "rep").astype(jnp.float32),
        lax.psum(parts[6].astype(jnp.bfloat16), "rep").astype(jnp.float32),
        lax.psum(parts[7].astype(jnp.bfloat16), "rep").astype(jnp.float32),
        lax.psum(parts[8].astype(jnp.bfloat16), "rep").astype(jnp.float32),
    )


def flat_body(
    tokens,
    segments,
    positions,
    norm1_gain,
    w_query,
    w_key,
    w_value,
    w_out,
    norm2_gain,
    w_gate,
    w_up,
    w_down,
    cotangent,
):
    seq_count = tokens.shape[0]
    local_len = tokens.shape[1]
    full_len = local_len * lax.axis_size("grp")
    row_count = seq_count * local_len
    group_size = H // KV
    score_scale = HD ** (-0.5)
    inputs = tokens.reshape(row_count, D).astype(jnp.float32)
    gain_in, query_full, key_full, value_full, out_full = fetch_attention(
        norm1_gain, w_query, w_key, w_value, w_out
    )
    scale_in = norm_scale(inputs)
    unit_in = inputs * scale_in
    normed_in = (unit_in * gain_in.astype(jnp.float32)).astype(jnp.bfloat16)
    query_raw = jnp.dot(normed_in, query_full, preferred_element_type=jnp.float32)
    key_raw = jnp.dot(normed_in, key_full, preferred_element_type=jnp.float32)
    value_raw = jnp.dot(normed_in, value_full, preferred_element_type=jnp.float32)
    cosine, sines = rotation_tables(positions, HD)
    query_rot = rotate(query_raw.reshape(seq_count, local_len, H, HD), cosine, sines).astype(
        jnp.bfloat16
    )
    key_rot = (
        rotate(key_raw.reshape(seq_count, local_len, KV, HD), cosine, sines)
        .astype(jnp.bfloat16)
        .reshape(seq_count, local_len, KV * HD)
    )
    value_low = value_raw.astype(jnp.bfloat16).reshape(seq_count, local_len, KV * HD)
    keys_all, values_all = (
        lax.all_gather(key_rot, "grp", axis=1, tiled=True),
        lax.all_gather(value_low, "grp", axis=1, tiled=True),
    )
    query_index = lax.axis_index("grp") * local_len + jnp.arange(local_len, dtype=jnp.int32)
    offsets = query_index[:, None] - jnp.arange(full_len, dtype=jnp.int32)[None, :]
    allowed = (
        (offsets >= 0)[None]
        & (offsets[None] <= positions[:, :, None])
        & ((segments[:, :, None] != 0) | (offsets == 0)[None])
    )
    query_heads = query_rot.reshape(seq_count, local_len, KV, group_size, HD).transpose(
        2, 0, 1, 3, 4
    )
    key_heads = keys_all.reshape(seq_count, full_len, KV, HD).transpose(2, 0, 1, 3)
    value_heads = values_all.reshape(seq_count, full_len, KV, HD).transpose(2, 0, 1, 3)

    def masked_scores(query_head, key_head):
        scores = (
            jnp.einsum("bqgd,bjd->bgqj", query_head, key_head, preferred_element_type=jnp.float32)
            * score_scale
        )
        return jnp.where(allowed[:, None], scores, NEGATIVE)

    def head_forward(items):
        query_head, key_head, value_head = items
        masked = masked_scores(query_head, key_head)
        peak = jnp.max(masked, axis=-1, keepdims=True)
        exponent = jnp.exp(masked - peak)
        summed = jnp.sum(exponent, axis=-1, keepdims=True)
        softmaxed = exponent / summed
        attended = jnp.einsum(
            "bgqj,bjd->bqgd",
            softmaxed.astype(jnp.bfloat16),
            value_head,
            preferred_element_type=jnp.float32,
        )
        return (attended, peak + jnp.log(summed))

    attended, log_totals = lax.map(head_forward, (query_heads, key_heads, value_heads))
    attn_low = attended.transpose(1, 2, 0, 3, 4).reshape(row_count, H * HD).astype(jnp.bfloat16)
    middle = inputs + jnp.dot(attn_low, out_full, preferred_element_type=jnp.float32)
    gain_mid, gate_full, up_full, down_full = fetch_mlp(norm2_gain, w_gate, w_up, w_down)
    scale_mid = norm_scale(middle)
    unit_mid = middle * scale_mid
    normed_mid = (unit_mid * gain_mid.astype(jnp.float32)).astype(jnp.bfloat16)
    gate_raw = jnp.dot(normed_mid, gate_full, preferred_element_type=jnp.float32)
    up_raw = jnp.dot(normed_mid, up_full, preferred_element_type=jnp.float32)
    sigmoid_gate = jax.nn.sigmoid(gate_raw)
    hidden_low = (gate_raw * sigmoid_gate * up_raw).astype(jnp.bfloat16)
    output = (
        (middle + jnp.dot(hidden_low, down_full, preferred_element_type=jnp.float32))
        .astype(jnp.bfloat16)
        .reshape(tokens.shape)
    )
    gain_mid, gate_full, up_full, down_full = fetch_mlp(norm2_gain, w_gate, w_up, w_down)
    cot_low = cotangent.reshape(row_count, D)
    hidden_delta = against(cot_low, down_full)
    gate_delta = (
        hidden_delta * up_raw * sigmoid_gate * (1.0 + gate_raw * (1.0 - sigmoid_gate))
    ).astype(jnp.bfloat16)
    upward_delta = (hidden_delta * gate_raw * sigmoid_gate).astype(jnp.bfloat16)
    columns = normed_mid
    gate_part = lax.psum_scatter(
        contract_rows(columns, gate_delta).astype(jnp.bfloat16),
        "grp",
        scatter_dimension=0,
        tiled=True,
    ).astype(jnp.float32)
    columns = normed_mid
    up_part = lax.psum_scatter(
        contract_rows(columns, upward_delta).astype(jnp.bfloat16),
        "grp",
        scatter_dimension=0,
        tiled=True,
    ).astype(jnp.float32)
    columns = hidden_low
    down_part = lax.psum_scatter(
        contract_rows(columns, cot_low).astype(jnp.bfloat16), "grp", scatter_dimension=0, tiled=True
    ).astype(jnp.float32)
    gate_grad, up_grad, down_grad = (gate_part, up_part, down_part)
    normed_mid_delta = against(gate_delta, gate_full) + against(upward_delta, up_full)
    gain_mid_term = jnp.sum(normed_mid_delta * unit_mid, axis=0)
    scaled_mid = normed_mid_delta * gain_mid.astype(jnp.float32)
    middle_delta = cot_low.astype(jnp.float32) + scale_mid * (
        scaled_mid - unit_mid * jnp.mean(scaled_mid * unit_mid, axis=-1, keepdims=True)
    )
    gain_in, query_full, key_full, value_full, out_full = fetch_attention(
        norm1_gain, w_query, w_key, w_value, w_out
    )
    out_delta = middle_delta.astype(jnp.bfloat16)
    out_term = contract_rows(attn_low, out_delta)
    attn_delta = against(out_delta, out_full).astype(jnp.bfloat16)
    attn_heads = attn_delta.reshape(seq_count, local_len, KV, group_size, HD).transpose(
        2, 0, 1, 3, 4
    )

    def head_backward(items):
        query_head, key_head, value_head, log_total, attn_head = items
        masked = masked_scores(query_head, key_head)
        softmaxed = jnp.exp(masked - log_total)
        prob_delta = jnp.einsum(
            "bqgd,bjd->bgqj", attn_head, value_head, preferred_element_type=jnp.float32
        )
        value_delta = jnp.einsum(
            "bgqj,bqgd->bjd",
            softmaxed.astype(jnp.bfloat16),
            attn_head,
            preferred_element_type=jnp.float32,
        )
        score_delta = (
            softmaxed * (prob_delta - jnp.sum(softmaxed * prob_delta, axis=-1, keepdims=True))
        ).astype(jnp.bfloat16)
        query_delta = (
            jnp.einsum("bgqj,bjd->bqgd", score_delta, key_head, preferred_element_type=jnp.float32)
            * score_scale
        )
        key_delta = (
            jnp.einsum(
                "bgqj,bqgd->bjd", score_delta, query_head, preferred_element_type=jnp.float32
            )
            * score_scale
        )
        return (query_delta, key_delta, value_delta)

    query_deltas, key_deltas, value_deltas = lax.map(
        head_backward, (query_heads, key_heads, value_heads, log_totals, attn_heads)
    )
    key_delta_all = key_deltas.transpose(1, 2, 0, 3).reshape(seq_count, full_len, KV * HD)
    value_delta_all = value_deltas.transpose(1, 2, 0, 3).reshape(seq_count, full_len, KV * HD)
    key_delta_own, value_delta_own = (
        lax.psum_scatter(
            key_delta_all.astype(jnp.bfloat16), "grp", scatter_dimension=1, tiled=True
        ).astype(jnp.float32),
        lax.psum_scatter(
            value_delta_all.astype(jnp.bfloat16), "grp", scatter_dimension=1, tiled=True
        ).astype(jnp.float32),
    )
    query_low = (
        rotate_back(
            query_deltas.transpose(1, 2, 0, 3, 4).reshape(seq_count, local_len, H, HD),
            cosine,
            sines,
        )
        .reshape(row_count, H * HD)
        .astype(jnp.bfloat16)
    )
    key_low = (
        rotate_back(key_delta_own.reshape(seq_count, local_len, KV, HD), cosine, sines)
        .reshape(row_count, KV * HD)
        .astype(jnp.bfloat16)
    )
    value_delta_low = value_delta_own.reshape(row_count, KV * HD).astype(jnp.bfloat16)
    query_term = contract_rows(normed_in, query_low)
    key_term = contract_rows(normed_in, key_low)
    value_term = contract_rows(normed_in, value_delta_low)
    normed_in_delta = (
        against(query_low, query_full)
        + against(key_low, key_full)
        + against(value_delta_low, value_full)
    )
    gain_in_term = jnp.sum(normed_in_delta * unit_in, axis=0)
    scaled_in = normed_in_delta * gain_in.astype(jnp.float32)
    input_grad = middle_delta + scale_in * (
        scaled_in - unit_in * jnp.mean(scaled_in * unit_in, axis=-1, keepdims=True)
    )
    norm1_part, norm2_part, query_part, key_part, value_part, out_part = (
        lax.psum_scatter(
            gain_in_term.astype(jnp.bfloat16), "grp", scatter_dimension=0, tiled=True
        ).astype(jnp.float32),
        lax.psum_scatter(
            gain_mid_term.astype(jnp.bfloat16), "grp", scatter_dimension=0, tiled=True
        ).astype(jnp.float32),
        lax.psum_scatter(
            query_term.astype(jnp.bfloat16), "grp", scatter_dimension=0, tiled=True
        ).astype(jnp.float32),
        lax.psum_scatter(
            key_term.astype(jnp.bfloat16), "grp", scatter_dimension=0, tiled=True
        ).astype(jnp.float32),
        lax.psum_scatter(
            value_term.astype(jnp.bfloat16), "grp", scatter_dimension=0, tiled=True
        ).astype(jnp.float32),
        lax.psum_scatter(
            out_term.astype(jnp.bfloat16), "grp", scatter_dimension=0, tiled=True
        ).astype(jnp.float32),
    )
    (
        norm1_grad,
        norm2_grad,
        query_grad,
        key_grad,
        value_grad,
        out_grad,
        gate_grad,
        up_grad,
        down_grad,
    ) = replica_all(
        (
            norm1_part,
            norm2_part,
            query_part,
            key_part,
            value_part,
            out_part,
            gate_grad,
            up_grad,
            down_grad,
        )
    )
    return (
        output,
        input_grad.reshape(tokens.shape),
        norm1_grad,
        query_grad,
        key_grad,
        value_grad,
        out_grad,
        norm2_grad,
        gate_grad,
        up_grad,
        down_grad,
    )


def on_device(
    tokens,
    segments,
    positions,
    norm1_gain,
    w_query,
    w_key,
    w_value,
    w_out,
    norm2_gain,
    w_gate,
    w_up,
    w_down,
    cotangent,
):
    results = flat_body(
        tokens,
        segments,
        positions,
        norm1_gain,
        w_query,
        w_key,
        w_value,
        w_out,
        norm2_gain,
        w_gate,
        w_up,
        w_down,
        cotangent,
    )
    return results


def solution(mesh):
    in_specs = (
        P("rep", "grp", None),
        P("rep", "grp"),
        P("rep", "grp"),
        P("grp"),
        P("grp", None),
        P("grp", None),
        P("grp", None),
        P("grp", None),
        P("grp"),
        P("grp", None),
        P("grp", None),
        P("grp", None),
        P("rep", "grp", None),
    )
    out_specs = (
        P("rep", "grp", None),
        P("rep", "grp", None),
        P("grp"),
        P("grp", None),
        P("grp", None),
        P("grp", None),
        P("grp", None),
        P("grp"),
        P("grp", None),
        P("grp", None),
        P("grp", None),
    )
    return jax.shard_map(
        on_device, mesh=mesh, in_specs=in_specs, out_specs=out_specs, check_vma=False
    )
```

profile of v0, /device:TPU:0, one launch (start us, length us, event | category | flops | bytes accessed | tf_op | source)
XLA Modules:
  0.0 614.8 jit_solution(3722437577382787025)
XLA Ops:
  7.2 17.6 %all_gather.43 = bf16[512,512]{1,0:T(8,128)(2,1)S(1)} all-gather(bf16[128,512]{1,0:T(8,128)(2,1)} %param.23), channel_id=1, replica_groups=mesh['rep'=8,'grp'=4] {'grp'}, dimensions={0}, use_global_device_ids=true | all-gather | bytes 655360 | tf_op jit(solution)/shard_map/all_gather | solution.py:62
  24.8 11.8 %all-gather.1 = bf16[4,1,128]{2,1,0:T(2,128)(2,1)S(1)} all-gather(bf16[1,1,128]{2,1,0:T(2,128)(2,1)} %bitcast.349), channel_id=1, replica_groups=mesh['rep'=8,'grp'=4] {'grp'}, dimensions={0}, use_global_device_ids=true | all-gather | bytes 1280 | tf_op jit(solution)/shard_map/all_gather | solution.py:59
  37.8 2.0 convolution_convert_fusion.8
  39.9 19.2 %all_gather.47 = bf16[512,512]{1,0:T(8,128)(2,1)S(1)} all-gather(bf16[128,512]{1,0:T(8,128)(2,1)S(1)} %copy-done.27), channel_id=1, replica_groups=mesh['rep'=8,'grp'=4] {'grp'}, dimensions={0}, use_global_device_ids=true | all-gather | bytes 655360 | tf_op jit(solution)/shard_map/all_gather | solution.py:60
  59.4 19.7 %all_gather.45 = bf16[512,512]{1,0:T(8,128)(2,1)S(1)} all-gather(bf16[128,512]{1,0:T(8,128)(2,1)S(1)} %copy-done.28), channel_id=1, replica_groups=mesh['rep'=8,'grp'=4] {'grp'}, dimensions={0}, use_global_device_ids=true | all-gather | bytes 655360 | tf_op jit(solution)/shard_map/all_gather | solution.py:61
  84.0 17.9 %all_gather.48 = bf16[512,512]{1,0:T(8,128)(2,1)S(1)} all-gather(bf16[128,512]{1,0:T(8,128)(2,1)S(1)} %copy-done.29), channel_id=1, replica_groups=mesh['rep'=8,'grp'=4] {'grp'}, dimensions={0}, use_global_device_ids=true | all-gather | bytes 655360 | tf_op jit(solution)/shard_map/all_gather | solution.py:63
  101.9 9.7 %all-gather.2 = bf16[4,1,128]{2,1,0:T(2,128)(2,1)S(1)} all-gather(bf16[1,1,128]{2,1,0:T(2,128)(2,1)S(1)} %bitcast.350), channel_id=1, replica_groups=mesh['rep'=8,'grp'=4] {'grp'}, dimensions={0}, use_global_device_ids=true | all-gather | bytes 1280 | tf_op jit(solution)/shard_map/all_gather | solution.py:69
  112.3 2.3 copy.43
  114.6 2.0 copy.46
  116.7 2.7 copy.47
  119.4 26.0 %while.30 = (s32[]{:T(128)}, bf16[8,1,256,1,64]{2,4,3,1,0:T(8,128)(2,1)}, f32[8,1,1,256,1]{3,4,2,1,0:T(1,128)}, bf16[8,1,1024,64]{3,2,1,0:T(8,128)(2,1)S(1)}, bf...) while((s32[]{:T(128)}, ...), condition=%wide.region_4.5_spmd.clone.clone, body=%wide.region_1.4_spmd.clone.sunk.clone | while | flops 71040768 | bytes 3783017 | solution.py:170
  148.5 3.0 fusion.103
  151.6 31.7 %all-gather.13.cloned.1.call-done = bf16[512,1376]{0,1:T(8,128)(2,1)} async-done(((bf16[128,1376]{0,1:T(8,128)(2,1)}), bf16[512,1376]{0,1:T(8,128)(2,1)}) %all-gather.13.cloned.1.call-update) | async-done | bytes 1409040 | tf_op jit(solution)/shard_map/all_gather | solution.py:71
  183.2 3.0 fusion.104
  186.2 30.8 %all-gather.15.cloned.1.call-done = bf16[1376,512]{1,0:T(8,128)(2,1)} async-done(((bf16[344,512]{1,0:T(8,128)(2,1)}), bf16[1376,512]{1,0:T(8,128)(2,1)}) %all-gather.15.cloned.1.call-update) | async-done | bytes 1409040 | tf_op jit(solution)/shard_map/all_gather | solution.py:72
  217.1 4.0 multiply_convert_fusion.1
  226.2 60.1 %while.31 = (s32[]{:T(128)}, f32[8,1,256,1,64]{2,4,3,1,0:T(8,128)S(1)}, bf16[8,1,1024,64]{2,3,1,0:T(8,128)(2,1)}, bf16[8,1,1024,64]{2,3,1,0:T(8,128)(2,1)}, bf16...) while((s32[]{:T(128)}, ...), condition=%wide.region_9.10_spmd.clone.clone, body=%wide.region_7.9_spmd.clone.sunk.clone | while | flops 172048128 | bytes 9384321 | solution.py:256
  297.7 15.1 %reduce-scatter.14.cloned.1.call-done = bf16[1,256,512]{1,2,0:T(8,128)(2,1)} async-done(((bf16[1,1024,512]{1,2,0:T(8,128)(2,1)}), bf16[1,256,512]{1,2,0:T(8,128)(2,1)}) %reduce-scatter.14.cloned.1.call-update) | async-done | bytes 262160 | tf_op jit(solution)/shard_map/reduce_scatter | solution.py:262
  317.7 23.2 %reduce-scatter.16.cloned.1.call-done = bf16[1,256,512]{1,2,0:T(8,128)(2,1)} async-done(((bf16[1,1024,512]{1,2,0:T(8,128)(2,1)}), bf16[1,256,512]{1,2,0:T(8,128)(2,1)}) %reduce-scatter.16.cloned.1.call-update) | async-done | bytes 262160 | tf_op jit(solution)/shard_map/reduce_scatter | solution.py:265
  340.9 2.2 convolution_convert_fusion.4
  344.4 2.7 fusion.63
  347.5 27.7 %reduce-scatter.28.cloned.1.call-done = bf16[128,1376]{1,0:T(8,128)(2,1)} async-done(((bf16[512,1376]{1,0:T(8,128)(2,1)}), bf16[128,1376]{1,0:T(8,128)(2,1)}) %reduce-scatter.28.cloned.1.call-update) | async-done | bytes 352272
  375.2 1.9 copy.56
  377.1 32.6 %reduce-scatter.30.cloned.1.call-done = bf16[128,1376]{1,0:T(8,128)(2,1)} async-done(((bf16[512,1376]{1,0:T(8,128)(2,1)}), bf16[128,1376]{1,0:T(8,128)(2,1)}) %reduce-scatter.30.cloned.1.call-update) | async-done | bytes 352272
  411.6 21.4 %reduce-scatter.24.cloned.1.call-done = bf16[128,512]{1,0:T(8,128)(2,1)} async-done(((bf16[512,512]{1,0:T(8,128)(2,1)}), bf16[128,512]{1,0:T(8,128)(2,1)}) %reduce-scatter.24.cloned.1.call-update) | async-done | bytes 131088 | tf_op jit(solution)/shard_map/reduce_scatter | solution.py:313
  433.1 33.5 %reduce-scatter.26.cloned.1.call-done = bf16[344,512]{1,0:T(8,128)(2,1)} async-done(((bf16[1376,512]{1,0:T(8,128)(2,1)}), bf16[344,512]{1,0:T(8,128)(2,1)}) %reduce-scatter.26.cloned.1.call-update) | async-done | bytes 352272 | tf_op jit(solution)/shard_map/reduce_scatter | solution.py:208
  466.5 23.4 %reduce-scatter.18.cloned.1.call-done = bf16[128,512]{1,0:T(8,128)(2,1)} async-done(((bf16[512,512]{1,0:T(8,128)(2,1)}), bf16[128,512]{1,0:T(8,128)(2,1)}) %reduce-scatter.18.cloned.1.call-update) | async-done | bytes 131088 | tf_op jit(solution)/shard_map/reduce_scatter | solution.py:304
  489.9 23.0 %reduce-scatter.20.cloned.1.call-done = bf16[128,512]{1,0:T(8,128)(2,1)} async-done(((bf16[512,512]{1,0:T(8,128)(2,1)}), bf16[128,512]{1,0:T(8,128)(2,1)}) %reduce-scatter.20.cloned.1.call-update) | async-done | bytes 131088 | tf_op jit(solution)/shard_map/reduce_scatter | solution.py:307
  512.9 22.9 %reduce-scatter.22.cloned.1.call-done = bf16[128,512]{1,0:T(8,128)(2,1)} async-done(((bf16[512,512]{1,0:T(8,128)(2,1)}), bf16[128,512]{1,0:T(8,128)(2,1)}) %reduce-scatter.22.cloned.1.call-update) | async-done | bytes 131088 | tf_op jit(solution)/shard_map/reduce_scatter | solution.py:310
  537.5 8.6 %all-reduce.4 = (bf16[512]{0:T(512)(128)(2,1)S(1)}, bf16[512]{0:T(512)(128)(2,1)S(1)}) all-reduce(bf16[512]{0:T(512)(128)(2,1)S(1)} %get-tuple-element.225, bf16[512]{0:T(512)(128)(2,1)S(1)} %copy-done.30), channel_id=5, replica_groups=mesh['rep'=8,'grp'=4] {'grp'}, use_global_device_ids=true, to_apply=%region_14.15.clone | all-reduce | flops 1024 | bytes 4096
  546.3 12.0 %all-reduce.2 = (bf16[128]{0:T(256)(128)(2,1)S(1)}, bf16[128]{0:T(256)(128)(2,1)S(1)}) all-reduce(bf16[128]{0:T(256)(128)(2,1)S(1)} %dynamic-slice.1, bf16[128]{0:T(256)(128)(2,1)S(1)} %dynamic-slice.3), channel_id=1, replica_groups=mesh['rep'=8,'grp'=4] {'rep'}, use_global_device_ids=true, to_apply=%region_15.16 | all-reduce | flops 256 | bytes 1024 | tf_op jit(solution)/shard_map/psum | solution.py:78
  560.3 38.6 %all-reduce.7.cloned.1.call-done = (bf16[128,512]{1,0:T(8,128)(2,1)}, bf16[128,512]{1,0:T(8,128)(2,1)}, bf16[128,512]{1,0:T(8,128)(2,1)}, bf16[128,512]{1,0:T(8,...) async-done(((bf16[128,512]{1,0:T(8,128)(2,1)}, bf16[128,512]{1,0:T(8,128)(2,1)}, bf16[128,512]{1,0:T(8,128)(2,1)}, ...) | async-done | bytes 1581072 | tf_op jit(solution)/shard_map/psum | solution.py:80
  (268 shorter events, 133.4 us)
Async XLA Ops:
  7.2 32.7 %copy-start.27 = (bf16[128,512]{1,0:T(8,128)(2,1)S(1)}, bf16[128,512]{1,0:T(8,128)(2,1)}, u32[]{:S(2)}) copy-start(bf16[128,512]{1,0:T(8,128)(2,1)} %param.21) | copy-start | bytes 393220
  7.2 105.1 %all-gather.17.cloned.1.call-start = ((), (), s32[]{:S(2)}) async-start(), calls=%async_computation.20 | async-start | bytes 1310720 | tf_op jit(solution)/shard_map/all_gather | solution.py:133
  24.8 15.0 %copy-start.14 = (bf16[512,512]{1,0:T(8,128)(2,1)}, bf16[512,512]{1,0:T(8,128)(2,1)S(1)}, u32[]{:S(2)}) copy-start(bf16[512,512]{1,0:T(8,128)(2,1)S(1)} %all_gather.43) | copy-start | bytes 1572868
  37.7 21.6 %copy-start.31 = (s32[1,256]{1,0:T(1,128)S(1)}, s32[1,256]{1,0:T(1,128)}, u32[]{:S(2)}) copy-start(s32[1,256]{1,0:T(1,128)} %param.19) | copy-start | bytes 3076
  37.8 21.6 %copy-start.28 = (bf16[128,512]{1,0:T(8,128)(2,1)S(1)}, bf16[128,512]{1,0:T(8,128)(2,1)}, u32[]{:S(2)}) copy-start(bf16[128,512]{1,0:T(8,128)(2,1)} %param.22) | copy-start | bytes 393220
  39.8 76.8 %all-gather.9.cloned.1.call-start = ((), (), s32[]{:S(2)}) async-start(), calls=%async_computation.9 | async-start | bytes 1310720 | tf_op jit(solution)/shard_map/all_gather | solution.py:132
  59.1 20.6 %copy-start.4 = (bf16[512,512]{1,0:T(8,128)(2,1)}, bf16[512,512]{1,0:T(8,128)(2,1)S(1)}, u32[]{:S(2)}) copy-start(bf16[512,512]{1,0:T(8,128)(2,1)S(1)} %all_gather.47) | copy-start | bytes 1572868
  59.1 20.2 %copy-start = (bf16[1,256,512]{2,1,0:T(8,128)(2,1)S(1)}, bf16[1,256,512]{2,1,0:T(8,128)(2,1)}, u32[]{:S(2)}) copy-start(bf16[1,256,512]{2,1,0:T(8,128)(2,1)} %param.17) | copy-start | bytes 786436
  80.5 21.4 %copy-start.33 = (bf16[128]{0:T(256)(128)(2,1)S(1)}, bf16[128]{0:T(256)(128)(2,1)}, u32[]{:S(2)}) copy-start(bf16[128]{0:T(256)(128)(2,1)} %param.25) | copy-start | bytes 772
  81.3 67.2 %all-gather.11.cloned.1.call-start = ((), (), s32[]{:S(2)}) async-start(), calls=%async_computation.10 | async-start | bytes 1761280 | tf_op jit(solution)/shard_map/all_gather | solution.py:70
  82.0 101.2 %all-gather.13.cloned.1.call-start = ((), (), s32[]{:S(2)}) async-start(), calls=%async_computation.11 | async-start | bytes 1761280 | tf_op jit(solution)/shard_map/all_gather | solution.py:71
  82.6 134.4 %all-gather.15.cloned.1.call-start = ((), (), s32[]{:S(2)}) async-start(), calls=%async_computation.12 | async-start | bytes 1761280 | tf_op jit(solution)/shard_map/all_gather | solution.py:72
  83.2 229.6 %reduce-scatter.14.cloned.1.call-start = ((), (), s32[]{:S(2)}) async-start(), calls=%async_computation.13 | async-start | bytes 1310720 | tf_op jit(solution)/shard_map/reduce_scatter | solution.py:262
  101.9 44.8 %copy-start.6 = (bf16[512,512]{1,0:T(8,128)(2,1)}, bf16[512,512]{1,0:T(8,128)(2,1)S(1)}, u32[]{:S(2)}) copy-start(bf16[512,512]{1,0:T(8,128)(2,1)S(1)} %all_gather.48) | copy-start | bytes 1572868
  145.4 6.1 copy-start.35
  145.4 6.1 copy-start.38
  151.6 65.5 %copy-start.16 = (bf16[1,256,512]{2,1,0:T(8,128)(2,1)S(1)}, bf16[1,256,512]{2,1,0:T(8,128)(2,1)}, u32[]{:S(2)}) copy-start(bf16[1,256,512]{2,1,0:T(8,128)(2,1)} %param.29) | copy-start | bytes 786436
  186.2 34.8 %copy-start.2 = (bf16[512,1376]{0,1:T(8,128)(2,1)S(1)}, bf16[512,1376]{0,1:T(8,128)(2,1)}, u32[]{:S(2)}) copy-start(bf16[512,1376]{0,1:T(8,128)(2,1)} %all-gather.11.cloned.1.call-done) | copy-start | bytes 4227076
  286.4 54.5 %reduce-scatter.16.cloned.1.call-start = ((), (), s32[]{:S(2)}) async-start(), calls=%async_computation.14 | async-start | bytes 1310720 | tf_op jit(solution)/shard_map/reduce_scatter | solution.py:265
  287.1 88.1 %reduce-scatter.28.cloned.1.call-start = ((), (), s32[]{:S(2)}) async-start(), calls=%async_computation.21 | async-start | bytes 1802240
  290.4 119.3 %reduce-scatter.30.cloned.1.call-start = ((), (), s32[]{:S(2)}) async-start(), calls=%async_computation.22 | async-start | bytes 1802240
  293.7 139.4 %reduce-scatter.24.cloned.1.call-start = ((), (), s32[]{:S(2)}) async-start(), calls=%async_computation.18 | async-start | bytes 655360 | tf_op jit(solution)/shard_map/reduce_scatter | solution.py:313
  295.7 170.8 %reduce-scatter.26.cloned.1.call-start = ((), (), s32[]{:S(2)}) async-start(), calls=%async_computation.19 | async-start | bytes 1761280 | tf_op jit(solution)/shard_map/reduce_scatter | solution.py:208
  297.6 16.2 %copy-start.26 = (f32[256,32]{0,1:T(8,128)S(1)}, f32[256,32]{0,1:T(8,128)}, u32[]{:S(2)}) copy-start(f32[256,32]{0,1:T(8,128)} %copy-done.25) | copy-start | bytes 98308
  297.7 192.2 %reduce-scatter.18.cloned.1.call-start = ((), (), s32[]{:S(2)}) async-start(), calls=%async_computation.15 | async-start | bytes 655360 | tf_op jit(solution)/shard_map/reduce_scatter | solution.py:304
  316.3 196.6 %reduce-scatter.20.cloned.1.call-start = ((), (), s32[]{:S(2)}) async-start(), calls=%async_computation.16 | async-start | bytes 655360 | tf_op jit(solution)/shard_map/reduce_scatter | solution.py:307
  316.4 26.8 %copy-start.37 = (u32[32]{0:T(128)S(1)}, u32[32]{0:T(128)}, u32[]{:S(2)}) copy-start(u32[32]{0:T(128)} %constant.83) | copy-start | bytes 388
  317.6 218.1 %reduce-scatter.22.cloned.1.call-start = ((), (), s32[]{:S(2)}) async-start(), calls=%async_computation.17 | async-start | bytes 655360 | tf_op jit(solution)/shard_map/reduce_scatter | solution.py:310
  343.1 255.8 %all-reduce.7.cloned.1.call-start = ((), (), s32[]{:S(2)}) async-start(), calls=%async_computation.23 | async-start | bytes 3162112 | tf_op jit(solution)/shard_map/psum | solution.py:80
  598.9 6.7 %copy-start.24 = (bf16[128,1376]{0,1:T(8,128)(2,1)S(1)}, bf16[128,1376]{0,1:T(8,128)(2,1)}, u32[]{:S(2)}) copy-start(bf16[128,1376]{0,1:T(8,128)(2,1)} %get-tuple-element.275) | copy-start | bytes 1056772
  598.9 7.6 %copy-start.23 = (bf16[128,1376]{0,1:T(8,128)(2,1)S(1)}, bf16[128,1376]{0,1:T(8,128)(2,1)}, u32[]{:S(2)}) copy-start(bf16[128,1376]{0,1:T(8,128)(2,1)} %get-tuple-element.276) | copy-start | bytes 1056772
  602.2 5.1 copy-start.22
  (23 other events, 43.6 us)
Sparse Core Ops, SparseCore 0:
  40.0 36.5 all-gather.16
  81.4 31.7 all-gather.8
  114.8 33.6 all-gather.10
  149.9 33.2 all-gather.12
  184.6 32.3 all-gather.14
  286.5 26.2 reduce-scatter.13
  315.1 25.7 reduce-scatter.15
  343.2 31.9 reduce-scatter.27
  377.5 32.1 reduce-scatter.29
  412.4 20.6 reduce-scatter.23
  435.4 31.1 reduce-scatter.25
  469.2 20.6 reduce-scatter.17
  492.7 20.1 reduce-scatter.19
  515.6 20.1 reduce-scatter.21
  539.8 59.1 all-reduce.6
where the time goes:
time: 617 us; the launch traced here: 615 us
  waiting for transfers between devices  327 us (53%)
  blocking collectives  116 us (19%)
  matrix products  104 us (17%)
  local copies, waits for them, and re-layouts  30.9 us (5%)
  other arithmetic  20.6 us (3%)
  between operations  15.1 us (2%)
    unnamed x17, waiting for transfers between devices  62.9 us
    psum x1, waiting for transfers between devices, replica_all(): lax.psum(parts[2].astype(jnp.bfloat16), 'rep').astype(jnp.float32)  38.6 us
    reduce_scatter x1, waiting for transfers between devices, flat_body(): lax.psum_scatter(contract_rows(columns, cot_low).astype(jnp.bfloat16), 'g...  33.5 us
    all_gather x1, waiting for transfers between devices, fetch_mlp(): lax.all_gather(w_up, 'grp', axis=0, tiled=True)  31.7 us
    all_gather x1, waiting for transfers between devices, fetch_mlp(): lax.all_gather(w_down, 'grp', axis=0, tiled=True)  30.8 us
    dot_general x16, matrix products, masked_scores(): jnp.einsum('bqgd,bjd->bgqj', query_head, key_head, preferred_element_type...  25.2 us
    reduce_scatter x1, waiting for transfers between devices, flat_body(): lax.psum_scatter(query_term.astype(jnp.bfloat16), 'grp', scatter_dimensio...  23.4 us
    reduce_scatter x1, waiting for transfers between devices, flat_body(): lax.psum_scatter(value_delta_all.astype(jnp.bfloat16), 'grp', scatter_dim...  23.2 us
  transfers between devices with their start and end apart: 15, of which 13 were waited for; matrix products, arithmetic and copies ran while one was open for 12% of the time, Pallas kernels for 0%

commit v1 on v0

--- a/solution.py
+++ b/solution.py
@@ -9,6 +9,27 @@
 HD = 64
 EPSILON = 1e-05
 NEGATIVE = -1e30
+
+
+def ring_gather(x, axis, dim):
+    length, place, width = (lax.axis_size(axis), lax.axis_index(axis), x.shape[dim])
+    right = [(i, (i + 1) % length) for i in range(length)]
+    left = [(i, (i - 1) % length) for i in range(length)]
+    out = jnp.zeros((*x.shape[:dim], length * width, *x.shape[dim + 1 :]), x.dtype)
+    out = lax.dynamic_update_slice_in_dim(out, x, place * width, axis=dim)
+    from_left = from_right = x
+    half = length // 2
+    for step in range(1, half + 1):
+        from_left = lax.ppermute(from_left, axis, right)
+        out = lax.dynamic_update_slice_in_dim(
+            out, from_left, (place - step) % length * width, axis=dim
+        )
+        if step < length - half:
+            from_right = lax.ppermute(from_right, axis, left)
+            out = lax.dynamic_update_slice_in_dim(
+                out, from_right, (place + step) % length * width, axis=dim
+            )
+    return out
 
 
 def norm_scale(values):
@@ -57,7 +78,7 @@
 def fetch_attention(norm1_gain, w_query, w_key, w_value, w_out):
     return (
         lax.all_gather(norm1_gain, "grp", axis=0, tiled=True),
-        lax.all_gather(w_query, "grp", axis=0, tiled=True),
+        ring_gather(w_query, "grp", 0),
         lax.all_gather(w_key, "grp", axis=0, tiled=True),
         lax.all_gather(w_value, "grp", axis=0, tiled=True),
         lax.all_gather(w_out, "grp", axis=0, tiled=True),

time: 617 us -> 613 us (level)
  blocking collectives: 116 us -> 95.6 us
  waiting for transfers between devices: 327 us -> 336 us
    all_gather x1 -> x0, blocking collectives: 19.2 us -> none  [fetch_attention(): lax.all_gather(w_query, 'grp', axis=0, tiled=True)]
    ppermute x0 -> x3, waiting for transfers between devices: none -> 10.2 us  [the longest x2 10.2 us: ring_gather(): from_left = lax.ppermute(from_left, axis, right)]
    unnamed x89 -> x88, local copies, waits for them, and re-layouts: 18.3 us -> 18.5 us
  transfers between devices with their start and end apart: 15 -> 18, of which waited for: 13 -> 14; matrix products, arithmetic and copies ran while one was open for 12% -> 12% of each run, Pallas kernels for 0% -> 0%
where the time goes in v1:
time: 613 us; the launch traced here: 611 us
  waiting for transfers between devices  336 us (55%)
  matrix products  105 us (17%)
  blocking collectives  95.6 us (16%)
  local copies, waits for them, and re-layouts  31.5 us (5%)
  other arithmetic  20.6 us (3%)
  between operations  15.2 us (2%)
    unnamed x17, waiting for transfers between devices  62.2 us
    psum x1, waiting for transfers between devices, replica_all(): lax.psum(parts[2].astype(jnp.bfloat16), 'rep').astype(jnp.float32)  38.6 us
    reduce_scatter x1, waiting for transfers between devices, flat_body(): lax.psum_scatter(contract_rows(columns, cot_low).astype(jnp.bfloat16), 'g...  33.5 us
    all_gather x1, waiting for transfers between devices, fetch_mlp(): lax.all_gather(w_up, 'grp', axis=0, tiled=True)  31.6 us
    all_gather x1, waiting for transfers between devices, fetch_mlp(): lax.all_gather(w_down, 'grp', axis=0, tiled=True)  30.8 us
    dot_general x16, matrix products, masked_scores(): jnp.einsum('bqgd,bjd->bgqj', query_head, key_head, preferred_element_type...  25.2 us
    reduce_scatter x1, waiting for transfers between devices, flat_body(): lax.psum_scatter(query_term.astype(jnp.bfloat16), 'grp', scatter_dimensio...  23.3 us
    reduce_scatter x1, waiting for transfers between devices, flat_body(): lax.psum_scatter(value_delta_all.astype(jnp.bfloat16), 'grp', scatter_dim...  23.2 us
  transfers between devices with their start and end apart: 18, of which 14 were waited for; matrix products, arithmetic and copies ran while one was open for 12% of the time, Pallas kernels for 0%

profile of v1, /device:TPU:0, one launch (start us, length us, event | category | flops | bytes accessed | tf_op | source)
XLA Modules:
  0.0 610.6 jit_solution(10199262282425821649)
XLA Ops:
  7.2 3.1 collective-permute-start
  10.3 2.1 collective-permute-start.1
  12.4 17.3 %all_gather.39 = bf16[512,512]{1,0:T(8,128)(2,1)S(1)} all-gather(bf16[128,512]{1,0:T(8,128)(2,1)} %param.23), channel_id=1, replica_groups=mesh['rep'=8,'grp'=4] {'grp'}, dimensions={0}, use_global_device_ids=true | all-gather | bytes 655360 | tf_op jit(solution)/shard_map/all_gather | solution.py:83
  29.7 10.5 %all-gather.1 = bf16[4,1,128]{2,1,0:T(2,128)(2,1)S(1)} all-gather(bf16[1,1,128]{2,1,0:T(2,128)(2,1)} %bitcast.347), channel_id=1, replica_groups=mesh['rep'=8,'grp'=4] {'grp'}, dimensions={0}, use_global_device_ids=true | all-gather | bytes 1280 | tf_op jit(solution)/shard_map/all_gather | solution.py:80
  41.4 2.1 convolution_convert_fusion.8
  43.5 19.2 %all_gather.41 = bf16[512,512]{1,0:T(8,128)(2,1)S(1)} all-gather(bf16[128,512]{1,0:T(8,128)(2,1)S(1)} %copy-done.26), channel_id=1, replica_groups=mesh['rep'=8,'grp'=4] {'grp'}, dimensions={0}, use_global_device_ids=true | all-gather | bytes 655360 | tf_op jit(solution)/shard_map/all_gather | solution.py:82
  64.3 10.2 %collective-permute-done.2 = bf16[128,512]{1,0:T(8,128)(2,1)S(1)} collective-permute-done((bf16[128,512]{1,0:T(8,128)(2,1)S(1)}, bf16[128,512]{1,0:T(8,128)(2,1)S(1)}, u32[]{:S(2)}, u32[]{:S(2)}) %collective-permute-start.2) | collective-permute-done | bytes 131104 | tf_op jit(solution)/shard_map/ppermute | solution.py:23
  79.0 18.0 %all_gather.43 = bf16[512,512]{1,0:T(8,128)(2,1)S(1)} all-gather(bf16[128,512]{1,0:T(8,128)(2,1)S(1)} %copy-done.27), channel_id=1, replica_groups=mesh['rep'=8,'grp'=4] {'grp'}, dimensions={0}, use_global_device_ids=true | all-gather | bytes 655360 | tf_op jit(solution)/shard_map/all_gather | solution.py:84
  96.9 10.1 %all-gather.2 = bf16[4,1,128]{2,1,0:T(2,128)(2,1)S(1)} all-gather(bf16[1,1,128]{2,1,0:T(2,128)(2,1)S(1)} %bitcast.348), channel_id=1, replica_groups=mesh['rep'=8,'grp'=4] {'grp'}, dimensions={0}, use_global_device_ids=true | all-gather | bytes 1280 | tf_op jit(solution)/shard_map/all_gather | solution.py:90
  107.7 2.3 copy.51
  112.1 2.7 copy.58
  114.8 26.1 %while.30 = (s32[]{:T(128)}, bf16[8,1,256,1,64]{2,4,3,1,0:T(8,128)(2,1)}, f32[8,1,1,256,1]{3,4,2,1,0:T(1,128)}, bf16[8,1,1024,64]{3,2,1,0:T(8,128)(2,1)S(1)}, bf...) while((s32[]{:T(128)}, ...), condition=%wide.region_4.5_spmd.clone.clone, body=%wide.region_1.4_spmd.clone.sunk.clone | while | flops 71040768 | bytes 3783017 | solution.py:191
  145.3 3.0 fusion.105
  148.4 31.6 %all-gather.13.cloned.1.call-done = bf16[512,1376]{0,1:T(8,128)(2,1)} async-done(((bf16[128,1376]{0,1:T(8,128)(2,1)}), bf16[512,1376]{0,1:T(8,128)(2,1)}) %all-gather.13.cloned.1.call-update) | async-done | bytes 1409040 | tf_op jit(solution)/shard_map/all_gather | solution.py:92
  180.0 3.0 fusion.106
  183.0 30.8 %all-gather.15.cloned.1.call-done = bf16[1376,512]{1,0:T(8,128)(2,1)} async-done(((bf16[344,512]{1,0:T(8,128)(2,1)}), bf16[1376,512]{1,0:T(8,128)(2,1)}) %all-gather.15.cloned.1.call-update) | async-done | bytes 1409040 | tf_op jit(solution)/shard_map/all_gather | solution.py:93
  213.8 4.0 multiply_convert_fusion.1
  223.0 60.3 %while.31 = (s32[]{:T(128)}, f32[8,1,256,1,64]{2,4,3,1,0:T(8,128)S(1)}, bf16[8,1,1024,64]{2,3,1,0:T(8,128)(2,1)}, bf16[8,1,1024,64]{2,3,1,0:T(8,128)(2,1)}, bf16...) while((s32[]{:T(128)}, ...), condition=%wide.region_9.10_spmd.clone.clone, body=%wide.region_7.9_spmd.clone.sunk.clone | while | flops 172048128 | bytes 9384321 | solution.py:277
  294.5 15.3 %reduce-scatter.14.cloned.1.call-done = bf16[1,256,512]{1,2,0:T(8,128)(2,1)} async-done(((bf16[1,1024,512]{1,2,0:T(8,128)(2,1)}), bf16[1,256,512]{1,2,0:T(8,128)(2,1)}) %reduce-scatter.14.cloned.1.call-update) | async-done | bytes 262160 | tf_op jit(solution)/shard_map/reduce_scatter | solution.py:283
  314.7 23.2 %reduce-scatter.16.cloned.1.call-done = bf16[1,256,512]{1,2,0:T(8,128)(2,1)} async-done(((bf16[1,1024,512]{1,2,0:T(8,128)(2,1)}), bf16[1,256,512]{1,2,0:T(8,128)(2,1)}) %reduce-scatter.16.cloned.1.call-update) | async-done | bytes 262160 | tf_op jit(solution)/shard_map/reduce_scatter | solution.py:286
  337.9 2.2 convolution_convert_fusion.4
  341.4 2.6 fusion.64
  345.2 27.0 %reduce-scatter.28.cloned.1.call-done = bf16[128,1376]{1,0:T(8,128)(2,1)} async-done(((bf16[512,1376]{1,0:T(8,128)(2,1)}), bf16[128,1376]{1,0:T(8,128)(2,1)}) %reduce-scatter.28.cloned.1.call-update) | async-done | bytes 352272
  374.1 32.6 %reduce-scatter.30.cloned.1.call-done = bf16[128,1376]{1,0:T(8,128)(2,1)} async-done(((bf16[512,1376]{1,0:T(8,128)(2,1)}), bf16[128,1376]{1,0:T(8,128)(2,1)}) %reduce-scatter.30.cloned.1.call-update) | async-done | bytes 352272
  408.6 20.9 %reduce-scatter.24.cloned.1.call-done = bf16[128,512]{1,0:T(8,128)(2,1)} async-done(((bf16[512,512]{1,0:T(8,128)(2,1)}), bf16[128,512]{1,0:T(8,128)(2,1)}) %reduce-scatter.24.cloned.1.call-update) | async-done | bytes 131088 | tf_op jit(solution)/shard_map/reduce_scatter | solution.py:334
  429.4 33.5 %reduce-scatter.26.cloned.1.call-done = bf16[344,512]{1,0:T(8,128)(2,1)} async-done(((bf16[1376,512]{1,0:T(8,128)(2,1)}), bf16[344,512]{1,0:T(8,128)(2,1)}) %reduce-scatter.26.cloned.1.call-update) | async-done | bytes 352272 | tf_op jit(solution)/shard_map/reduce_scatter | solution.py:229
  462.9 23.3 %reduce-scatter.18.cloned.1.call-done = bf16[128,512]{1,0:T(8,128)(2,1)} async-done(((bf16[512,512]{1,0:T(8,128)(2,1)}), bf16[128,512]{1,0:T(8,128)(2,1)}) %reduce-scatter.18.cloned.1.call-update) | async-done | bytes 131088 | tf_op jit(solution)/shard_map/reduce_scatter | solution.py:325
  486.3 23.0 %reduce-scatter.20.cloned.1.call-done = bf16[128,512]{1,0:T(8,128)(2,1)} async-done(((bf16[512,512]{1,0:T(8,128)(2,1)}), bf16[128,512]{1,0:T(8,128)(2,1)}) %reduce-scatter.20.cloned.1.call-update) | async-done | bytes 131088 | tf_op jit(solution)/shard_map/reduce_scatter | solution.py:328
  509.2 22.2 %reduce-scatter.22.cloned.1.call-done = bf16[128,512]{1,0:T(8,128)(2,1)} async-done(((bf16[512,512]{1,0:T(8,128)(2,1)}), bf16[128,512]{1,0:T(8,128)(2,1)}) %reduce-scatter.22.cloned.1.call-update) | async-done | bytes 131088 | tf_op jit(solution)/shard_map/reduce_scatter | solution.py:331
  533.3 8.6 %all-reduce.4 = (bf16[512]{0:T(512)(128)(2,1)S(1)}, bf16[512]{0:T(512)(128)(2,1)S(1)}) all-reduce(bf16[512]{0:T(512)(128)(2,1)S(1)} %get-tuple-element.225, bf16[512]{0:T(512)(128)(2,1)S(1)} %copy-done.29), channel_id=5, replica_groups=mesh['rep'=8,'grp'=4] {'grp'}, use_global_device_ids=true, to_apply=%region_14.15.clone | all-reduce | flops 1024 | bytes 4096
  542.1 12.0 %all-reduce.2 = (bf16[128]{0:T(256)(128)(2,1)S(1)}, bf16[128]{0:T(256)(128)(2,1)S(1)}) all-reduce(bf16[128]{0:T(256)(128)(2,1)S(1)} %dynamic-slice.1, bf16[128]{0:T(256)(128)(2,1)S(1)} %dynamic-slice.3), channel_id=1, replica_groups=mesh['rep'=8,'grp'=4] {'rep'}, use_global_device_ids=true, to_apply=%region_15.16 | all-reduce | flops 256 | bytes 1024 | tf_op jit(solution)/shard_map/psum | solution.py:99
  556.1 38.6 %all-reduce.7.cloned.1.call-done = (bf16[128,512]{1,0:T(8,128)(2,1)}, bf16[128,512]{1,0:T(8,128)(2,1)}, bf16[128,512]{1,0:T(8,128)(2,1)}, bf16[128,512]{1,0:T(8,...) async-done(((bf16[128,512]{1,0:T(8,128)(2,1)}, bf16[128,512]{1,0:T(8,128)(2,1)}, bf16[128,512]{1,0:T(8,128)(2,1)}, ...) | async-done | bytes 1581072 | tf_op jit(solution)/shard_map/psum | solution.py:101
  (280 shorter events, 140.2 us)
Async XLA Ops:
  7.2 36.3 %copy-start.26 = (bf16[128,512]{1,0:T(8,128)(2,1)S(1)}, bf16[128,512]{1,0:T(8,128)(2,1)}, u32[]{:S(2)}) copy-start(bf16[128,512]{1,0:T(8,128)(2,1)} %param.22) | copy-start | bytes 393220
  7.2 55.5 %copy-start.30 = (s32[1,256]{1,0:T(1,128)S(1)}, s32[1,256]{1,0:T(1,128)}, u32[]{:S(2)}) copy-start(s32[1,256]{1,0:T(1,128)} %param.19) | copy-start | bytes 3076
  7.2 100.5 %all-gather.17.cloned.1.call-start = ((), (), s32[]{:S(2)}) async-start(), calls=%async_computation.20 | async-start | bytes 1310720 | tf_op jit(solution)/shard_map/all_gather | solution.py:154
  7.2 56.6 %collective-permute-start = (bf16[128,512]{1,0:T(8,128)(2,1)}, bf16[128,512]{1,0:T(8,128)(2,1)S(1)}, u32[]{:S(2)}, u32[]{:S(2)}) collective-permute-start(bf16[128,512]{1,0:T(8,128)(2,1)} %param.21), channel_id=1, source_target_pairs={{0,1},{1,2},{2,3},{3,0},{4,5},{5,6},{6,7},{7,4},{8,9},{9,10},{10,1... | collective-permute-start | bytes 393224 | tf_op jit(solution)/shard_map/ppermute | solution.py:23
  10.3 53.8 %collective-permute-start.1 = (bf16[128,512]{1,0:T(8,128)(2,1)}, bf16[128,512]{1,0:T(8,128)(2,1)S(1)}, u32[]{:S(2)}, u32[]{:S(2)}) collective-permute-start(bf16[128,512]{1,0:T(8,128)(2,1)} %param.21), channel_id=1, source_target_pairs={{0,3},{1,0},{2,1},{3,2},{4,7},{5,4},{6,5},{7,6},{8,11},{9,8},{10,9... | collective-permute-start | bytes 393224 | tf_op jit(solution)/shard_map/ppermute | solution.py:28
  29.7 11.6 %copy-start.13 = (bf16[512,512]{1,0:T(8,128)(2,1)}, bf16[512,512]{1,0:T(8,128)(2,1)S(1)}, u32[]{:S(2)}) copy-start(bf16[512,512]{1,0:T(8,128)(2,1)S(1)} %all_gather.39) | copy-start | bytes 1572868
  41.3 21.8 %copy-start = (bf16[1,256,512]{2,1,0:T(8,128)(2,1)S(1)}, bf16[1,256,512]{2,1,0:T(8,128)(2,1)}, u32[]{:S(2)}) copy-start(bf16[1,256,512]{2,1,0:T(8,128)(2,1)} %param.17) | copy-start | bytes 786436
  43.5 20.1 %copy-start.28 = (bf16[128,512]{1,0:T(8,128)(2,1)S(1)}, bf16[128,512]{1,0:T(8,128)(2,1)}, u32[]{:S(2)}) copy-start(bf16[128,512]{1,0:T(8,128)(2,1)} %param.21) | copy-start | bytes 393220
  43.5 68.6 %all-gather.9.cloned.1.call-start = ((), (), s32[]{:S(2)}) async-start(), calls=%async_computation.9 | async-start | bytes 1310720 | tf_op jit(solution)/shard_map/all_gather | solution.py:153
  63.1 12.0 %copy-start.24 = (f32[256,32]{0,1:T(8,128)}, f32[256,32]{0,1:T(8,128)S(1)}, u32[]{:S(2)}) copy-start(f32[256,32]{0,1:T(8,128)S(1)} %get-tuple-element.300) | copy-start | bytes 98308
  64.0 10.5 %collective-permute-start.2 = (bf16[128,512]{1,0:T(8,128)(2,1)S(1)}, bf16[128,512]{1,0:T(8,128)(2,1)S(1)}, u32[]{:S(2)}, u32[]{:S(2)}) collective-permute-start(bf16[128,512]{1,0:T(8,128)(2,1)S(1)} %collective-permute-done), channel_id=1, source_target_pairs={{0,1},{1,2},{2,3},{3,0},{4,5},{5,6},{6,7},{7,4},{8,9},{9,10},{10,1... | collective-permute-start | bytes 393224 | tf_op jit(solution)/shard_map/ppermute | solution.py:23
  75.5 21.4 %copy-start.32 = (bf16[128]{0:T(256)(128)(2,1)S(1)}, bf16[128]{0:T(256)(128)(2,1)}, u32[]{:S(2)}) copy-start(bf16[128]{0:T(256)(128)(2,1)} %param.25) | copy-start | bytes 772
  76.3 69.1 %all-gather.11.cloned.1.call-start = ((), (), s32[]{:S(2)}) async-start(), calls=%async_computation.10 | async-start | bytes 1761280 | tf_op jit(solution)/shard_map/all_gather | solution.py:91
  77.0 103.0 %all-gather.13.cloned.1.call-start = ((), (), s32[]{:S(2)}) async-start(), calls=%async_computation.11 | async-start | bytes 1761280 | tf_op jit(solution)/shard_map/all_gather | solution.py:92
  77.6 136.3 %all-gather.15.cloned.1.call-start = ((), (), s32[]{:S(2)}) async-start(), calls=%async_computation.12 | async-start | bytes 1761280 | tf_op jit(solution)/shard_map/all_gather | solution.py:93
  78.2 231.6 %reduce-scatter.14.cloned.1.call-start = ((), (), s32[]{:S(2)}) async-start(), calls=%async_computation.13 | async-start | bytes 1310720 | tf_op jit(solution)/shard_map/reduce_scatter | solution.py:283
  96.9 45.3 %copy-start.6 = (bf16[512,512]{1,0:T(8,128)(2,1)}, bf16[512,512]{1,0:T(8,128)(2,1)S(1)}, u32[]{:S(2)}) copy-start(bf16[512,512]{1,0:T(8,128)(2,1)S(1)} %all_gather.43) | copy-start | bytes 1572868
  148.4 65.5 %copy-start.15 = (bf16[1,256,512]{2,1,0:T(8,128)(2,1)S(1)}, bf16[1,256,512]{2,1,0:T(8,128)(2,1)}, u32[]{:S(2)}) copy-start(bf16[1,256,512]{2,1,0:T(8,128)(2,1)} %param.29) | copy-start | bytes 786436
  183.0 34.8 %copy-start.2 = (bf16[512,1376]{0,1:T(8,128)(2,1)S(1)}, bf16[512,1376]{0,1:T(8,128)(2,1)}, u32[]{:S(2)}) copy-start(bf16[512,1376]{0,1:T(8,128)(2,1)} %all-gather.11.cloned.1.call-done) | copy-start | bytes 4227076
  283.3 54.6 %reduce-scatter.16.cloned.1.call-start = ((), (), s32[]{:S(2)}) async-start(), calls=%async_computation.14 | async-start | bytes 1310720 | tf_op jit(solution)/shard_map/reduce_scatter | solution.py:286
  284.1 88.1 %reduce-scatter.28.cloned.1.call-start = ((), (), s32[]{:S(2)}) async-start(), calls=%async_computation.21 | async-start | bytes 1802240
  287.3 119.3 %reduce-scatter.30.cloned.1.call-start = ((), (), s32[]{:S(2)}) async-start(), calls=%async_computation.22 | async-start | bytes 1802240
  290.6 138.8 %reduce-scatter.24.cloned.1.call-start = ((), (), s32[]{:S(2)}) async-start(), calls=%async_computation.18 | async-start | bytes 655360 | tf_op jit(solution)/shard_map/reduce_scatter | solution.py:334
  292.7 170.2 %reduce-scatter.26.cloned.1.call-start = ((), (), s32[]{:S(2)}) async-start(), calls=%async_computation.19 | async-start | bytes 1761280 | tf_op jit(solution)/shard_map/reduce_scatter | solution.py:229
  294.4 16.4 %copy-start.25 = (f32[256,32]{0,1:T(8,128)S(1)}, f32[256,32]{0,1:T(8,128)}, u32[]{:S(2)}) copy-start(f32[256,32]{0,1:T(8,128)} %copy-done.24) | copy-start | bytes 98308
  294.4 191.8 %reduce-scatter.18.cloned.1.call-start = ((), (), s32[]{:S(2)}) async-start(), calls=%async_computation.15 | async-start | bytes 655360 | tf_op jit(solution)/shard_map/reduce_scatter | solution.py:325
  313.3 195.9 %reduce-scatter.20.cloned.1.call-start = ((), (), s32[]{:S(2)}) async-start(), calls=%async_computation.16 | async-start | bytes 655360 | tf_op jit(solution)/shard_map/reduce_scatter | solution.py:328
  313.4 26.8 %copy-start.36 = (u32[32]{0:T(128)S(1)}, u32[32]{0:T(128)}, u32[]{:S(2)}) copy-start(u32[32]{0:T(128)} %constant.122) | copy-start | bytes 388
  314.6 216.8 %reduce-scatter.22.cloned.1.call-start = ((), (), s32[]{:S(2)}) async-start(), calls=%async_computation.17 | async-start | bytes 655360 | tf_op jit(solution)/shard_map/reduce_scatter | solution.py:331
  340.1 254.6 %all-reduce.7.cloned.1.call-start = ((), (), s32[]{:S(2)}) async-start(), calls=%async_computation.23 | async-start | bytes 3162112 | tf_op jit(solution)/shard_map/psum | solution.py:101
  345.2 186.3 %copy-start.14 = (bf16[512,512]{1,0:T(8,128)(2,1)S(1)}, bf16[512,512]{1,0:T(8,128)(2,1)}, u32[]{:S(2)}) copy-start(bf16[512,512]{1,0:T(8,128)(2,1)} %copy-done.13) | copy-start | bytes 1572868
  345.2 186.3 %copy-start.18 = (bf16[1,256,512]{1,2,0:T(8,128)(2,1)S(1)}, bf16[1,256,512]{1,2,0:T(8,128)(2,1)}, u32[]{:S(2)}) copy-start(bf16[1,256,512]{1,2,0:T(8,128)(2,1)} %reduce-scatter.16.cloned.1.call-done) | copy-start | bytes 786436
  (25 other events, 68.0 us)
Sparse Core Ops, SparseCore 0:
  43.6 32.7 all-gather.16
  78.5 31.0 all-gather.8
  111.2 34.0 all-gather.10
  146.7 33.2 all-gather.12
  181.4 32.3 all-gather.14
  283.4 26.2 reduce-scatter.13
  312.1 25.7 reduce-scatter.15
  340.2 31.8 reduce-scatter.27
  374.5 32.1 reduce-scatter.29
  408.8 20.6 reduce-scatter.23
  431.8 31.1 reduce-scatter.25
  465.6 20.5 reduce-scatter.17
  489.1 20.0 reduce-scatter.19
  511.4 20.0 reduce-scatter.21
  535.5 59.1 all-reduce.6
